TPU v7x, 1024 devices: a whole 4x4x32 slice. The times are simulated.
1024 devices in a mesh: sfc: 128 (over x, z), grp: 8 (over y, core).
Axes of the slice: x: 4, y: 4, z: 32, core: 2. Of those that a mesh axis runs over, the one named last changes fastest.
Arguments:
- tracers: float32 [16, 4, 8, 196608], P(None, None, None, ('sfc', 'grp')), may hold values from 0.05 to 60, as said below
- send_counts: int32 [128, 8, 24], P('sfc', 'grp'), may hold values from 1 to 256, 3072 in all within a row
- point_order: int32 [128, 8, 3072], P('sfc', 'grp'), may hold values from 0 to 3071, each once within a row
- depart_elem: int32 [128, 8, 3, 8, 256], P('sfc', 'grp'), may hold values from 0 to 191
- depart_coords: float32 [128, 8, 2, 3, 8, 256], P('sfc', 'grp'), may hold values from -1 to 1
Outputs:
- transported: float32 [16, 4, 8, 196608], P(None, None, None, ('sfc', 'grp'))
Inputs may be any that keep to these rules, and one draw needn't show every extreme that they name: `send_counts`: each row lists, for the 24 owner blocks of one device, how many of its arrival points depart from that owner's elements; a row sums to 3072, and its largest entry is exactly 256. `point_order`: each row is a permutation of the device's arrival points. `tracers`: Positive.
All inputs are finite; a program needn't handle non-finite values.
Results may differ from a plain program's by a relative error of at most 0.0003.
Values sent between devices are 32-bit elements; how exact they have to be, the bound alone decides.
A program may use at most 64 MiB of HBM per device.

v0:
```python
import jax
import jax.numpy as jnp
from jax import lax
from jax.sharding import Mesh
from jax.sharding import PartitionSpec as P

SFC = ("sfc_0", "sfc_1")
GRP = ("grp_0", "grp_1")
SFC_GRP = ("sfc_0", "sfc_1", "grp_0", "grp_1")


NODE_COORD = (-1.0, -0.4472135954999579, 0.4472135954999579, 1.0)
NODE_WEIGHT = (1.0 / 6.0, 5.0 / 6.0, 5.0 / 6.0, 1.0 / 6.0)


def passed_along(x, axis, by):
    devices = lax.axis_size(axis)
    return lax.ppermute(x, axis, [(i, (i + by) % devices) for i in range(devices)])


def split_up(x, dim, devices):
    dims = x.shape
    parts = x.reshape(*dims[:dim], devices, dims[dim] // devices, *dims[dim + 1 :])
    return jnp.moveaxis(parts, dim, 0)


def in_order(parts, dim):
    dims = list(parts.shape[1:])
    dims[dim] *= parts.shape[0]
    return jnp.moveaxis(parts, 0, dim).reshape(dims)


def moved_by_axis(parts, axes, order):
    inside = parts.shape[1:]
    filled = parts.reshape(*(lax.axis_size(a) for a in axes), *inside)
    for k in order:
        filled = lax.all_to_all(filled, axes[k], k, k, tiled=True)
    return filled.reshape(-1, *inside)


def exchange_by_chip(x, groups, order, split_dim, concat_dim):
    devices = lax.axis_size(groups[0]) * lax.axis_size(groups[1])
    parts = split_up(x, split_dim, devices)
    return in_order(moved_by_axis(parts, groups, order), concat_dim)


def over_axes(x, axes):
    for axis in axes:
        x = lax.psum(x, axis)
    return x


def lagrange(coordinate):
    basis_values = []
    for row_node in range(4):
        weighted = jnp.ones_like(coordinate)
        for other_node in range(4):
            if other_node != row_node:
                weighted = weighted * (
                    (coordinate - NODE_COORD[other_node])
                    / (NODE_COORD[row_node] - NODE_COORD[other_node])
                )
        basis_values.append(weighted)
    return basis_values


def interpolate(tracer_field, received):
    source_row = received[0].astype(jnp.int32)
    along_first = lagrange(received[1])
    along_second = lagrange(received[2])
    running_sum = None
    for row_node in range(4):
        for column_node in range(4):
            node_plane = jnp.take(tracer_field[4 * row_node + column_node], source_row, axis=1)
            weighted = (along_first[row_node] * along_second[column_node])[None, :] * node_plane
            if running_sum is None:
                running_sum, lower_bound, upper_bound = (weighted, node_plane, node_plane)
            else:
                running_sum = running_sum + weighted
                lower_bound = jnp.minimum(lower_bound, node_plane)
                upper_bound = jnp.maximum(upper_bound, node_plane)
    return jnp.clip(running_sum, lower_bound, upper_bound)


def quad_table():
    return jnp.array(
        [NODE_WEIGHT[a] * NODE_WEIGHT[b] for a in range(4) for b in range(4)], jnp.float32
    )


def edge_weight(node_line):
    return jnp.where((node_line == 0) | (node_line == 3), 1.0 / 6.0, 5.0 / 6.0).astype(jnp.float32)


def send_across(outgoing, shift_by):
    return passed_along(outgoing, SFC, shift_by)


def send_back(returned, shift_by):
    return passed_along(returned, SFC, shift_by)


def local(tracers, send_counts, point_order, depart_elem, depart_coords):
    node_count, levels, tracer_count, element_count = tracers.shape
    channels = levels * tracer_count
    tracer_field = tracers.reshape(node_count, channels, element_count)
    groups = lax.axis_size(GRP)
    counts = send_counts.reshape(-1)
    capacity = depart_elem.shape[-1]
    points = node_count * element_count
    offsets = jnp.cumsum(counts) - counts
    slot_index = jnp.arange(capacity, dtype=jnp.int32)
    in_use = slot_index[None, :] < counts[:, None]
    position = jnp.minimum(offsets[:, None] + slot_index[None, :], points - 1)
    target_point = jnp.where(in_use, point_order.reshape(-1)[position], points)
    total_slots = 3 * groups * capacity
    slot_of_point = (
        jnp.zeros((points,), jnp.int32)
        .at[target_point.reshape(-1)]
        .set(jnp.arange(total_slots, dtype=jnp.int32), mode="drop")
    )
    components = [
        depart_elem.reshape(1, 3, groups, capacity).astype(jnp.float32),
        depart_coords.reshape(2, 3, groups, capacity),
    ]
    node_number = jnp.minimum(target_point, points - 1) // element_count
    mass_share = jnp.where(
        in_use, edge_weight(node_number // 4) * edge_weight(node_number % 4), 0.0
    )
    components.append(mass_share.reshape(1, 3, groups, capacity))
    payload = jnp.concatenate(components, 0)
    stacked = jnp.stack(
        [send_across(payload[:, 0], -1), payload[:, 1], send_across(payload[:, 2], 1)], 1
    )
    arrived = lax.all_to_all(stacked, GRP, split_axis=2, concat_axis=2, tiled=True)
    flat_arrived = arrived.reshape(arrived.shape[0], -1)
    values = interpolate(tracer_field, flat_arrived)
    owned = jnp.sum(values * flat_arrived[3][None, :], axis=1)
    returned = exchange_by_chip(
        values.reshape(channels, 3, groups, capacity), ("grp_0", "grp_1"), (1, 0), 2, 2
    )
    collected = jnp.stack(
        [send_back(returned[:, 0], 1), returned[:, 1], send_back(returned[:, 2], -1)], 1
    )
    flat_collected = collected.reshape(channels, total_slots)
    slot_table = slot_of_point.reshape(node_count, element_count)
    limited = jnp.stack(
        [jnp.take(flat_collected, slot_table[node], axis=1) for node in range(16)], 0
    )
    quadrature = quad_table()
    old_part = jnp.sum(jnp.sum(tracer_field, axis=2) * quadrature[:, None], axis=0)
    old_mass, new_mass = (over_axes(old_part, SFC_GRP), over_axes(owned, SFC_GRP))
    corrected = limited * (old_mass / new_mass)[None, :, None]
    return corrected.reshape(node_count, levels, tracer_count, element_count)


def solution(mesh):
    split = Mesh(mesh.devices.reshape(4, 32, 4, 2), ("sfc_0", "sfc_1", "grp_0", "grp_1"))
    return jax.shard_map(
        local,
        mesh=split,
        in_specs=(
            P(None, None, None, SFC_GRP),
            P(SFC, GRP, None),
            P(SFC, GRP, None),
            P(SFC, GRP, None, None, None),
            P(SFC, GRP, None, None, None, None),
        ),
        out_specs=P(None, None, None, SFC_GRP),
        check_vma=False,
    )
```

profile of v0, /device:TPU:1, one launch (start us, length us, event | category | flops | bytes accessed | tf_op | source)
XLA Modules:
  0.0 636.6 jit_solution(11550368373809428933)
XLA Ops:
  1.7 34.3 %gather_fusion = s32[6144]{0:T(1024)S(1)} fusion(s32[3072]{0:T(1024)S(1)} %bitcast.403, s32[6144]{0:T(1024)S(1)} %broadcast_clamp_fusion), kind=kCustom, calls=%fused_computation.32 | custom fusion | bytes 73728 | tf_op jit(solution)/shard_map/gather | solution.py:115
  37.7 4.4 collective-permute-start.1
  42.1 19.0 %collective-permute-start = (f32[4,8,256]{2,0,1:T(4,128)S(1)}, f32[4,8,256]{2,0,1:T(4,128)S(1)}, u32[]{:S(2)}, u32[]{:S(2)}) collective-permute-start(f32[4,8,256]{2,0,1:T(4,128)S(1)} %get-tuple-element.40), channel_id=1, source_target_pairs={{0,1016},{8,0},{16,8},{24,16},{32,24},{40,32},{48,40},{56,48},{64,... | collective-permute-start | bytes 98312 | tf_op jit(solution)/shard_map/ppermute | solution.py:18
  61.3 23.0 %scatter_custom_fusion = s32[3072]{0:T(1024)S(1)} fusion(s32[6144]{0:T(1024)S(1)} %bitcast.452, s32[6144]{0:T(1024)S(1)} %iota.14, s32[]{:T(128)} %constant.107.clone.1), kind=kCustom, calls=%fused_computation.209 | custom fusion | bytes 12292 | tf_op jit(solution)/shard_map/scatter | solution.py:120
  86.7 5.4 all-to-all-start
  92.1 5.0 all-to-all-done
  97.2 20.9 %gather_fusion.1 = f32[6144,32]{1,0:T(8,128)} fusion(f32[32,192]{0,1:T(8,128)S(1)} %copy.311, s32[6144]{0:T(1024)S(1)} %fusion.21), kind=kCustom, calls=%fused_computation.clone | custom fusion | bytes 1597440 | tf_op jit(solution)/shard_map/jit(_take)/gather | solution.py:74
  120.5 20.9 %gather_fusion.2 = f32[6144,32]{1,0:T(8,128)} fusion(f32[32,192]{0,1:T(8,128)S(1)} %copy.313, s32[6144]{0:T(1024)S(1)} %fusion.21), kind=kCustom, calls=%fused_computation.2.clone | custom fusion | bytes 1597440 | tf_op jit(solution)/shard_map/jit(_take)/gather | solution.py:74
  143.7 20.9 %gather_fusion.3 = f32[6144,32]{1,0:T(8,128)} fusion(f32[32,192]{0,1:T(8,128)S(1)} %copy.315, s32[6144]{0:T(1024)S(1)} %fusion.21), kind=kCustom, calls=%fused_computation.3.clone | custom fusion | bytes 1597440 | tf_op jit(solution)/shard_map/jit(_take)/gather | solution.py:74
  167.8 20.9 %gather_fusion.4 = f32[6144,32]{1,0:T(8,128)} fusion(f32[32,192]{0,1:T(8,128)S(1)} %copy.317, s32[6144]{0:T(1024)S(1)} %fusion.21), kind=kCustom, calls=%fused_computation.4.clone | custom fusion | bytes 1597440 | tf_op jit(solution)/shard_map/jit(_take)/gather | solution.py:74
  191.8 20.9 %gather_fusion.5 = f32[6144,32]{1,0:T(8,128)} fusion(f32[32,192]{0,1:T(8,128)S(1)} %copy.319, s32[6144]{0:T(1024)S(1)} %fusion.21), kind=kCustom, calls=%fused_computation.5.clone | custom fusion | bytes 1597440 | tf_op jit(solution)/shard_map/jit(_take)/gather | solution.py:74
  215.8 20.9 %gather_fusion.6 = f32[6144,32]{1,0:T(8,128)} fusion(f32[32,192]{0,1:T(8,128)S(1)} %copy.321, s32[6144]{0:T(1024)S(1)} %fusion.21), kind=kCustom, calls=%fused_computation.6.clone | custom fusion | bytes 1597440 | tf_op jit(solution)/shard_map/jit(_take)/gather | solution.py:74
  239.8 20.9 %gather_fusion.7 = f32[6144,32]{1,0:T(8,128)} fusion(f32[32,192]{0,1:T(8,128)S(1)} %copy.323, s32[6144]{0:T(1024)S(1)} %fusion.21), kind=kCustom, calls=%fused_computation.7.clone | custom fusion | bytes 1597440 | tf_op jit(solution)/shard_map/jit(_take)/gather | solution.py:74
  263.9 20.9 %gather_fusion.8 = f32[6144,32]{1,0:T(8,128)} fusion(f32[32,192]{0,1:T(8,128)S(1)} %copy.325, s32[6144]{0:T(1024)S(1)} %fusion.21), kind=kCustom, calls=%fused_computation.8.clone | custom fusion | bytes 1597440 | tf_op jit(solution)/shard_map/jit(_take)/gather | solution.py:74
  287.8 20.9 %gather_fusion.9 = f32[6144,32]{1,0:T(8,128)} fusion(f32[32,192]{0,1:T(8,128)S(1)} %copy.327, s32[6144]{0:T(1024)S(1)} %fusion.21), kind=kCustom, calls=%fused_computation.9.clone | custom fusion | bytes 1597440 | tf_op jit(solution)/shard_map/jit(_take)/gather | solution.py:74
  311.8 20.9 %gather_fusion.10 = f32[6144,32]{1,0:T(8,128)} fusion(f32[32,192]{0,1:T(8,128)S(1)} %copy.329, s32[6144]{0:T(1024)S(1)} %fusion.21), kind=kCustom, calls=%fused_computation.10.clone | custom fusion | bytes 1597440 | tf_op jit(solution)/shard_map/jit(_take)/gather | solution.py:74
  335.9 20.9 %gather_fusion.11 = f32[6144,32]{1,0:T(8,128)} fusion(f32[32,192]{0,1:T(8,128)S(1)} %copy.331, s32[6144]{0:T(1024)S(1)} %fusion.21), kind=kCustom, calls=%fused_computation.11.clone | custom fusion | bytes 1597440 | tf_op jit(solution)/shard_map/jit(_take)/gather | solution.py:74
  359.9 20.9 %gather_fusion.12 = f32[6144,32]{1,0:T(8,128)} fusion(f32[32,192]{0,1:T(8,128)S(1)} %copy.333, s32[6144]{0:T(1024)S(1)} %fusion.21), kind=kCustom, calls=%fused_computation.12.clone | custom fusion | bytes 1597440 | tf_op jit(solution)/shard_map/jit(_take)/gather | solution.py:74
  383.9 20.9 %gather_fusion.13 = f32[6144,32]{1,0:T(8,128)} fusion(f32[32,192]{0,1:T(8,128)S(1)} %copy.335, s32[6144]{0:T(1024)S(1)} %fusion.21), kind=kCustom, calls=%fused_computation.13.clone | custom fusion | bytes 1597440 | tf_op jit(solution)/shard_map/jit(_take)/gather | solution.py:74
  407.9 20.9 %gather_fusion.14 = f32[6144,32]{1,0:T(8,128)} fusion(f32[32,192]{0,1:T(8,128)S(1)} %copy.337, s32[6144]{0:T(1024)S(1)} %fusion.21), kind=kCustom, calls=%fused_computation.14.clone | custom fusion | bytes 1597440 | tf_op jit(solution)/shard_map/jit(_take)/gather | solution.py:74
  431.9 20.9 %gather_fusion.15 = f32[6144,32]{1,0:T(8,128)} fusion(f32[32,192]{0,1:T(8,128)S(1)} %copy.339, s32[6144]{0:T(1024)S(1)} %fusion.21), kind=kCustom, calls=%fused_computation.15.clone | custom fusion | bytes 1597440 | tf_op jit(solution)/shard_map/jit(_take)/gather | solution.py:74
  456.0 20.9 %gather_fusion.16 = f32[6144,32]{1,0:T(8,128)} fusion(f32[32,192]{0,1:T(8,128)S(1)} %copy.341, s32[6144]{0:T(1024)S(1)} %fusion.21), kind=kCustom, calls=%fused_computation.16.clone | custom fusion | bytes 1597440 | tf_op jit(solution)/shard_map/jit(_take)/gather | solution.py:74
  476.9 3.2 copy.342
  480.6 5.0 multiply_reduce_fusion
  486.2 4.9 all_to_all.15
  492.1 3.5 all-to-all-start.2
  498.3 9.2 %all-to-all-done.2 = f32[4,2,32,3,1,256]{5,2,4,3,1,0:T(8,128)S(1)} async-done(((f32[4,2,32,3,1,256]{5,2,4,3,1,0:T(8,128)}), f32[4,2,32,3,1,256]{5,2,4,3,1,0:T(8,128)S(1)}, u32[]{:S(2)}, u32[]{:S(2)}) %all-to-all-start.2) | async-done | bytes 786464 | tf_op jit(solution)/shard_map/all_to_all | solution.py:37
  510.0 6.7 %collective-permute-start.3 = (f32[32,8,256]{2,1,0:T(8,128)S(1)}, f32[32,8,256]{2,1,0:T(8,128)S(1)}, u32[]{:S(2)}, u32[]{:S(2)}) collective-permute-start(f32[32,8,256]{2,1,0:T(8,128)S(1)} %get-tuple-element.18), channel_id=1, source_target_pairs={{0,1016},{8,0},{16,8},{24,16},{32,24},{40,32},{48,40},{56,48},{64,... | collective-permute-start | bytes 786440 | tf_op jit(solution)/shard_map/ppermute | solution.py:18
  518.0 6.0 all-reduce.2
  524.0 39.7 %all-reduce = (f32[32]{0:T(128)S(1)}, f32[32]{0:T(128)S(1)}) all-reduce(f32[32]{0:T(128)S(1)} %get-tuple-element.11, f32[32]{0:T(128)S(1)} %get-tuple-element.12), channel_id=1, replica_groups=mesh['sfc_0'=4,'sfc_1'=32,'grp_0'=4,'grp_1'=2] {'sfc_1'}, use_global_device_ids=true, to_apply=%region_5.8 | all-reduce | flops 64 | bytes 512 | tf_op jit(solution)/shard_map/psum | solution.py:49
  563.8 6.9 %all-reduce.1 = (f32[32]{0:T(128)S(1)}, f32[32]{0:T(128)S(1)}) all-reduce(f32[32]{0:T(128)S(1)} %get-tuple-element.6, f32[32]{0:T(128)S(1)} %get-tuple-element.8), channel_id=1, replica_groups=mesh['sfc_0'=4,'sfc_1'=32,'grp_0'=4,'grp_1'=2] {'grp_0'}, use_global_device_ids=true, to_apply=%region_6.9 | all-reduce | flops 64 | bytes 512 | tf_op jit(solution)/shard_map/psum | solution.py:49
  570.6 21.8 %all-reduce.3 = (f32[32]{0:T(128)S(1)}, f32[32]{0:T(128)S(1)}) all-reduce(f32[32]{0:T(128)S(1)} %get-tuple-element.9, f32[32]{0:T(128)S(1)} %get-tuple-element.10), channel_id=1, replica_groups=mesh['sfc_0'=4,'sfc_1'=32,'grp_0'=4,'grp_1'=2] {'grp_1'}, use_global_device_ids=true, to_apply=%region_7.10 | all-reduce | flops 64 | bytes 512 | tf_op jit(solution)/shard_map/psum | solution.py:49
  (197 shorter events, 103.1 us)
Async XLA Ops:
  0.0 1.7 copy-start
  1.7 34.9 %copy-start.8 = (s32[1,1,24]{2,1,0:T(1,128)S(1)}, s32[1,1,24]{2,1,0:T(1,128)}, u32[]{:S(2)}) copy-start(s32[1,1,24]{2,1,0:T(1,128)} %param.11) | copy-start | bytes 292
  1.7 35.8 %copy-start.6 = (f32[1,1,2,3,8,256]{5,4,3,2,1,0:T(8,128)S(1)}, f32[1,1,2,3,8,256]{5,4,3,2,1,0:T(8,128)}, u32[]{:S(2)}) copy-start(f32[1,1,2,3,8,256]{5,4,3,2,1,0:T(8,128)} %param.14) | copy-start | bytes 147460
  1.7 35.8 %copy-start.7 = (s32[1,1,3,8,256]{4,3,2,1,0:T(8,128)S(1)}, s32[1,1,3,8,256]{4,3,2,1,0:T(8,128)}, u32[]{:S(2)}) copy-start(s32[1,1,3,8,256]{4,3,2,1,0:T(8,128)} %param.13) | copy-start | bytes 73732
  1.7 59.3 %copy-start.4 = (f32[16,4,8,192]{3,2,1,0:T(8,128)S(1)}, f32[16,4,8,192]{3,2,1,0:T(8,128)}, u32[]{:S(2)}) copy-start(f32[16,4,8,192]{3,2,1,0:T(8,128)} %param.10) | copy-start | bytes 1179652
  37.7 48.3 %collective-permute-start.1 = (f32[4,8,256]{2,0,1:T(4,128)S(1)}, f32[4,8,256]{2,0,1:T(4,128)S(1)}, u32[]{:S(2)}, u32[]{:S(2)}) collective-permute-start(f32[4,8,256]{2,0,1:T(4,128)S(1)} %get-tuple-element.41), channel_id=1, source_target_pairs={{0,8},{8,16},{16,24},{24,32},{32,40},{40,48},{48,56},{56,64},{64,7... | collective-permute-start | bytes 98312 | tf_op jit(solution)/shard_map/ppermute | solution.py:18
  42.1 43.9 %collective-permute-start = (f32[4,8,256]{2,0,1:T(4,128)S(1)}, f32[4,8,256]{2,0,1:T(4,128)S(1)}, u32[]{:S(2)}, u32[]{:S(2)}) collective-permute-start(f32[4,8,256]{2,0,1:T(4,128)S(1)} %get-tuple-element.40), channel_id=1, source_target_pairs={{0,1016},{8,0},{16,8},{24,16},{32,24},{40,32},{48,40},{56,48},{64,... | collective-permute-start | bytes 98312 | tf_op jit(solution)/shard_map/ppermute | solution.py:18
  86.7 10.4 %all-to-all-start = ((f32[4,3,8,256]{3,0,1,2:T(4,128)}), f32[4,3,8,256]{3,0,1,2:T(4,128)S(1)}, u32[]{:S(2)}, u32[]{:S(2)}) async-start(f32[4,3,8,256]{3,0,1,2:T(4,128)} %pad_maximum_fusion.2), calls=%async_computation | async-start | bytes 196608 | tf_op jit(solution)/shard_map/all_to_all | solution.py:135
  476.9 3.7 copy-start.2
  476.9 3.7 copy-start.3
  486.1 9.5 %copy-start.5 = (f32[16,4,8,192]{3,2,1,0:T(8,128)S(1)}, f32[16,4,8,192]{3,2,1,0:T(8,128)}, u32[]{:S(2)}) copy-start(f32[16,4,8,192]{3,2,1,0:T(8,128)} %param.10) | copy-start | bytes 1179652
  486.1 12.1 %copy-start.11 = (f32[16]{0:T(128)S(1)}, f32[16]{0:T(128)}, u32[]{:S(2)}) copy-start(f32[16]{0:T(128)} %constant.131.clone) | copy-start | bytes 196
  492.1 15.5 %all-to-all-start.2 = ((f32[4,2,32,3,1,256]{5,2,4,3,1,0:T(8,128)}), f32[4,2,32,3,1,256]{5,2,4,3,1,0:T(8,128)S(1)}, u32[]{:S(2)}, u32[]{:S(2)}) async-start(f32[4,2,32,3,1,256]{5,2,4,3,1,0:T(8,128)} %copy.347), calls=%async_computation.2 | async-start | bytes 1572864 | tf_op jit(solution)/shard_map/all_to_all | solution.py:37
  508.1 84.4 %collective-permute-start.2 = (f32[32,8,256]{2,1,0:T(8,128)S(1)}, f32[32,8,256]{2,1,0:T(8,128)S(1)}, u32[]{:S(2)}, u32[]{:S(2)}) collective-permute-start(f32[32,8,256]{2,1,0:T(8,128)S(1)} %get-tuple-element.17), channel_id=1, source_target_pairs={{0,8},{8,16},{16,24},{24,32},{32,40},{40,48},{48,56},{56,64},{64,7... | collective-permute-start | bytes 786440 | tf_op jit(solution)/shard_map/ppermute | solution.py:18
  510.0 82.5 %collective-permute-start.3 = (f32[32,8,256]{2,1,0:T(8,128)S(1)}, f32[32,8,256]{2,1,0:T(8,128)S(1)}, u32[]{:S(2)}, u32[]{:S(2)}) collective-permute-start(f32[32,8,256]{2,1,0:T(8,128)S(1)} %get-tuple-element.18), channel_id=1, source_target_pairs={{0,1016},{8,0},{16,8},{24,16},{32,24},{40,32},{48,40},{56,48},{64,... | collective-permute-start | bytes 786440 | tf_op jit(solution)/shard_map/ppermute | solution.py:18
  595.4 7.6 %copy-start.10 = (pred[192]{0:T(512)(128)(4,1)S(1)}, pred[192]{0:T(512)(128)(4,1)}, u32[]{:S(2)}) copy-start(pred[192]{0:T(512)(128)(4,1)} %get-tuple-element.67) | copy-start | bytes 580
  595.4 9.2 %copy-start.9 = (pred[192]{0:T(512)(128)(4,1)S(1)}, pred[192]{0:T(512)(128)(4,1)}, u32[]{:S(2)}) copy-start(pred[192]{0:T(512)(128)(4,1)} %get-tuple-element.66) | copy-start | bytes 580
  605.4 31.2 %copy-start.1 = (s32[1,1,3072]{2,1,0:T(1,128)S(1)}, s32[1,1,3072]{2,1,0:T(1,128)}, u32[]{:S(2)}) copy-start(s32[1,1,3072]{2,1,0:T(1,128)} %param.12) | copy-start | bytes 36868
where the time goes:
time: 638 us; the launch traced here: 637 us
  local copies, waits for them, and re-layouts  481 us (75%)
  blocking collectives  79.3 us (12%)
  starting transfers between devices  40.8 us (6%)
  other arithmetic  20.5 us (3%)
  waiting for transfers between devices  14.2 us (2%)
    gather x32, local copies, waits for them, and re-layouts, interpolate(): jnp.take(tracer_field[4 * row_node + column_node], source_row, axis=1)  383 us
    psum x4, blocking collectives, over_axes(): x = lax.psum(x, axis)  74.4 us
    gather x3, local copies, waits for them, and re-layouts, local(): target_point = jnp.where(in_use, point_order.reshape(-1)[position], points)  34.3 us
    ppermute x4, starting transfers between devices, passed_along(): lax.ppermute(x, axis, [(i, (i + by) % devices) for i in range(devices)])  31.9 us
    scatter x1, local copies, waits for them, and re-layouts, local(): slot_of_point = jnp.zeros((points,), jnp.int32).at[target_point.reshape(-...  23 us
    unnamed x63, local copies, waits for them, and re-layouts  15.8 us
  transfers between devices with their start and end apart: 6, of which 2 were waited for; matrix products, arithmetic and copies ran while one was open for 5% of the time, Pallas kernels for 0%

commit v1 on v0

v1 whole, which is shorter than its diff:
```python
import jax
import jax.numpy as jnp
from jax import lax
from jax.experimental import pallas as pl
from jax.experimental.pallas import tpu as pltpu
from jax.sharding import PartitionSpec as P

NODE_COORD = (-1.0, -0.4472135954999579, 0.4472135954999579, 1.0)
SIDES = 3
MESH = pl.DeviceIdType.MESH


def lagrange(x):
    values = []
    for i in range(4):
        value = None
        for m in range(4):
            if m != i:
                term = (x - NODE_COORD[m]) * (1.0 / (NODE_COORD[i] - NODE_COORD[m]))
                value = term if value is None else value * term
        values.append(value)
    return values


def line_weight(line):
    return jnp.where((line == 0) | (line == 3), 1.0 / 6.0, 5.0 / 6.0).astype(jnp.float32)


def split_bf16(x):
    high = x.astype(jnp.bfloat16)
    return high, (x - high.astype(jnp.float32)).astype(jnp.bfloat16)


def diagonal(n, start):
    return lax.broadcasted_iota(jnp.int32, (n, 128), 0) + start == lax.broadcasted_iota(
        jnp.int32, (n, 128), 1
    )


def as_row(column, start):
    return jnp.sum(jnp.where(diagonal(column.shape[0], start), column, 0.0), axis=0, keepdims=True)


def as_column(row, n, start):
    return jnp.sum(jnp.where(diagonal(n, start), row, 0.0), axis=1, keepdims=True)


def prep_kernel(elements, counts_ref, order_ref, elem_ref, coord_ref, request_ref, point_ref, order_pad):
    peers, capacity = elem_ref.shape
    rows = order_ref.shape[0]
    order_pad[0:rows, :] = order_ref[...]
    order_pad[rows:, :] = jnp.zeros((order_pad.shape[0] - rows, 128), jnp.int32)
    lane = lax.broadcasted_iota(jnp.int32, (8, 128), 1)
    slot = lane + 128 * lax.broadcasted_iota(jnp.int32, (8, 128), 0)
    offset = jnp.int32(0)
    for k in range(peers):
        count = counts_ref[0, k]
        row, shift = offset // 128, offset % 128
        window = order_pad[pl.ds(row, 8), :]
        window = pltpu.roll(window, (128 - shift) % 128, 1)
        following = pltpu.roll(window, 7, 0)
        window = jnp.where(lane < 128 - shift, window, following)
        window = jnp.where(slot < count, window, -1)
        for part in range(capacity // 128):
            point_ref[k : k + 1, part * 128 : part * 128 + 128] = window[part : part + 1, :]
        offset = offset + count
    point = point_ref[...]
    node = jnp.floor((point.astype(jnp.float32) + 0.5) * (1.0 / elements)).astype(jnp.int32)
    share = jnp.where(point >= 0, line_weight(node // 4) * line_weight(node % 4), 0.0)
    element = elem_ref[...].astype(jnp.float32)
    for k in range(peers):
        request_ref[k, 0:1, :] = element[k : k + 1, :]
        request_ref[k, 1:2, :] = coord_ref[k : k + 1, :]
        request_ref[k, 2:3, :] = coord_ref[peers + k : peers + k + 1, :]
        request_ref[k, 3:4, :] = share[k : k + 1, :]


def split_field(field_ref, high_ref, low_ref, channels):
    nodes = field_ref.shape[0] // channels
    elements = field_ref.shape[1]
    rows, width = high_ref.shape
    high_ref[:, 128:] = jnp.zeros((rows, width - 128), jnp.bfloat16)
    low_ref[:, 128:] = jnp.zeros((rows, width - 128), jnp.bfloat16)
    old = least = most = None
    for n in range(nodes):
        plane = field_ref[n * channels : (n + 1) * channels, :]
        weight = (5.0 if n // 4 in (1, 2) else 1.0) * (5.0 if n % 4 in (1, 2) else 1.0) / 36.0
        old = plane * weight if old is None else old + plane * weight
        least = plane if least is None else jnp.minimum(least, plane)
        most = plane if most is None else jnp.maximum(most, plane)
        high, low = split_bf16(plane)
        high_ref[n * channels : (n + 1) * channels, 0:elements] = high
        low_ref[n * channels : (n + 1) * channels, 0:elements] = low
    for n, plane in ((nodes, least), (nodes + 1, most)):
        high, low = split_bf16(plane)
        high_ref[n * channels : (n + 1) * channels, 0:elements] = high
        low_ref[n * channels : (n + 1) * channels, 0:elements] = low
    return jnp.sum(old, axis=1, keepdims=True)


def interpolate(requests, blocks, value_ref, high_ref, low_ref, gathered_ref):
    channels, capacity = value_ref.shape[1:]
    width = high_ref.shape[1]
    nodes = high_ref.shape[0] // channels - 2
    element = jnp.concatenate([requests[b, 0:1, :] for b in blocks], 1).astype(jnp.int32)
    source = lax.broadcasted_iota(jnp.int32, (width, element.shape[1]), 0)
    chosen = jnp.where(source == element, 1.0, 0.0).astype(jnp.bfloat16)
    gathered_ref[...] = jnp.dot(
        high_ref[...], chosen, preferred_element_type=jnp.float32
    ) + jnp.dot(low_ref[...], chosen, preferred_element_type=jnp.float32)
    mass = None
    for i, b in enumerate(blocks):
        cols = slice(i * capacity, (i + 1) * capacity)
        first = lagrange(requests[b, 1:2, :])
        second = lagrange(requests[b, 2:3, :])
        total = None
        for n in range(nodes):
            term = (first[n // 4] * second[n % 4]) * gathered_ref[n * channels : (n + 1) * channels, cols]
            total = term if total is None else total + term
        total = jnp.maximum(total, gathered_ref[nodes * channels : (nodes + 1) * channels, cols])
        total = jnp.minimum(total, gathered_ref[(nodes + 1) * channels : (nodes + 2) * channels, cols])
        value_ref[b] = total
        part = total * requests[b, 3:4, :]
        mass = part if mass is None else mass + part
    return mass


def scatter(point_ref, blocks, returned, total_ref, masked_ref, elements):
    channels, capacity = returned.shape[1:]
    nodes = total_ref.shape[0] // channels
    width = total_ref.shape[1]
    point = jnp.concatenate([point_ref[pl.ds(b, 1), :] for b in blocks], 1)
    node = jnp.floor((point.astype(jnp.float32) + 0.5) * (1.0 / elements)).astype(jnp.int32)
    element = jnp.where(point >= 0, point - node * elements, -1)
    place = lax.broadcasted_iota(jnp.int32, (width, element.shape[1]), 0)
    spread = jnp.where(place == element, 1.0, 0.0).astype(jnp.bfloat16)
    value = jnp.concatenate([returned[b] for b in blocks], 1)
    high, low = split_bf16(value)
    for n in range(nodes):
        mask = jnp.where(node == n, 1.0, 0.0).astype(jnp.bfloat16)
        masked_ref[0, n * channels : (n + 1) * channels, :] = high * mask
        masked_ref[1, n * channels : (n + 1) * channels, :] = low * mask
    dims = (((1,), (1,)), ((), ()))
    total_ref[...] += lax.dot_general(
        masked_ref[0], spread, dims, preferred_element_type=jnp.float32
    ) + lax.dot_general(masked_ref[1], spread, dims, preferred_element_type=jnp.float32)


def step_kernel(
    sizes, request_ref, point_ref, field_ref, out_ref,
    asked, values, returned, high_ref, low_ref, gathered_ref, total_ref, masked_ref,
    parts, group_mass, line_mass, ring_mass,
    ask_sent, ask_got, back_sent, back_got, mass_sent, mass_got, known,
):
    lines, ring, groups = sizes
    peers, channels, capacity = values.shape
    elements = field_ref.shape[1]
    nodes = out_ref.shape[0] // channels
    sfc, grp = lax.axis_index("sfc"), lax.axis_index("grp")
    segments = lines * ring
    line, place = sfc // ring, sfc % ring

    def at(segment, group):
        return {"sfc": segment, "grp": group}

    def side(u):
        return (2 * (u // groups)) % SIDES

    def owner(u):
        return (sfc + side(u) - 1 + segments) % segments, (grp + 1 + u) % groups

    def asker(u):
        return (sfc - side(u) + 1 + segments) % segments, (grp - 1 - u + 4 * groups) % groups

    def on_line(i):
        return at(((line + i) % lines) * ring + place, grp)

    def on_ring(i):
        return at(line * ring + (place + i + ring) % ring, grp)

    def ask(u):
        segment, group = owner(u)
        return pltpu.make_async_remote_copy(
            request_ref.at[side(u) * groups + group],
            asked.at[side(u) * groups + grp],
            ask_sent.at[u], ask_got.at[u],
            device_id=at(segment, group), device_id_type=MESH,
        )

    def answer(u):
        segment, group = asker(u)
        return pltpu.make_async_remote_copy(
            values.at[side(u) * groups + group],
            returned.at[side(u) * groups + grp],
            back_sent.at[u], back_got.at[u],
            device_id=at(segment, group), device_id_type=MESH,
        )

    def mass_copy(stage, slots, mine, index, device):
        return pltpu.make_async_remote_copy(
            parts.at[stage], slots.at[mine],
            mass_sent.at[index], mass_got.at[index],
            device_id=device, device_id_type=MESH,
        )

    def group_copy(i):
        return mass_copy(0, group_mass, grp, i, at(sfc, (grp + i) % groups))

    def line_copy(i):
        return mass_copy(1, line_mass, line, groups + i, on_line(i))

    def ring_copy(i):
        return mass_copy(2, ring_mass, place, groups + lines + i, on_ring(i))

    def each(count, act, start=0):
        def body(i, carry):
            act(i)
            return carry
        lax.fori_loop(start, count, body, 0)

    def greet(device):
        pl.semaphore_signal(pltpu.get_barrier_semaphore(), inc=1, device_id=device, device_id_type=MESH)

    others = peers - 1
    each(others, lambda u: greet(at(*owner(u))))
    for i in range(1, lines):
        greet(on_line(i))
    for i in (1, -1):
        greet(on_ring(i))

    old = split_field(field_ref, high_ref, low_ref, channels)
    total_ref[...] = jnp.zeros_like(total_ref)
    asked[groups + grp] = request_ref[groups + grp]

    pl.semaphore_wait(pltpu.get_barrier_semaphore(), others + lines - 1 + 2)
    each(others, lambda u: ask(u).start())

    def tell(step):
        for i in (1 << step, -(1 << step)):
            pl.semaphore_signal(known.at[step], inc=1, device_id=on_ring(i), device_id_type=MESH)

    def hear(step):
        pl.semaphore_wait(known.at[step], 2)

    steps = 0
    while (2 << steps) < ring:
        steps += 1
    tell(0)
    for step in range(1, steps - 1):
        hear(step - 1)
        tell(step)

    PAIR = 2

    def work(j, mass):
        @pl.when(j > 0)
        def _():
            for i in range(PAIR):
                answer(PAIR * (j - 1) + i).start()

        for i in range(PAIR):
            @pl.when(PAIR * j + i < others)
            def _():
                ask(PAIR * j + i).wait_recv()

        blocks = [side(PAIR * j + i) * groups + asker(PAIR * j + i)[1] for i in range(PAIR)]
        return mass + interpolate(asked, blocks, values, high_ref, low_ref, gathered_ref)

    rounds = peers // PAIR
    new = jnp.zeros((channels, capacity), jnp.float32)
    new = lax.fori_loop(0, rounds // 2, work, new)
    hear(steps - 2)
    tell(steps - 1)
    new = lax.fori_loop(rounds // 2, rounds, work, new)
    new = jnp.sum(new, axis=1, keepdims=True)
    parts[0] = as_row(old, 0) + as_row(new, channels)
    returned[groups + grp] = values[groups + grp]
    for u in range(PAIR * (rounds - 1), others):
        answer(u).start()
    group_mass[grp] = parts[0]
    each(groups, lambda i: group_copy(i).start(), 1)

    def put(j, carry):
        for i in range(PAIR):
            @pl.when(PAIR * j + i < others)
            def _():
                answer(PAIR * j + i).wait_recv()

        blocks = [side(PAIR * j + i) * groups + owner(PAIR * j + i)[1] for i in range(PAIR)]
        scatter(point_ref, blocks, returned, total_ref, masked_ref, elements)
        return carry

    third = rounds // 4
    lax.fori_loop(0, third, put, 0)
    each(groups, lambda i: group_copy(i).wait_recv(), 1)
    parts[1] = jnp.sum(group_mass[...], axis=0)
    line_mass[line] = parts[1]
    each(others, lambda u: ask(u).wait_send())
    each(lines, lambda i: line_copy(i).start(), 1)
    lax.fori_loop(third, 2 * third, put, 0)
    each(lines, lambda i: line_copy(i).wait_recv(), 1)
    parts[2] = jnp.sum(line_mass[...], axis=0)
    ring_mass[place] = parts[2]
    hear(steps - 1)
    each(ring, lambda i: ring_copy(i).start(), 1)
    lax.fori_loop(2 * third, rounds, put, 0)
    each(ring, lambda i: ring_copy(i).wait_recv(), 1)
    masses = jnp.sum(ring_mass[...], axis=0)
    factor = as_column(masses, channels, 0) / as_column(masses, channels, channels)
    for n in range(nodes):
        rows = slice(n * channels, (n + 1) * channels)
        out_ref[rows, :] = total_ref[rows, 0:elements] * factor
    each(others, lambda u: answer(u).wait_send())
    each(groups, lambda i: group_copy(i).wait_send(), 1)
    each(lines, lambda i: line_copy(i).wait_send(), 1)
    each(ring, lambda i: ring_copy(i).wait_send(), 1)


def in_vmem(count):
    return [pl.BlockSpec(memory_space=pltpu.VMEM)] * count


def prep(counts, order, elem, coords, elements):
    peers, capacity = elem.shape
    rows = order.shape[0]
    return pl.pallas_call(
        lambda *refs: prep_kernel(elements, *refs),
        out_shape=(
            jax.ShapeDtypeStruct((peers, 4, capacity), jnp.float32),
            jax.ShapeDtypeStruct((peers, capacity), jnp.int32),
        ),
        in_specs=[pl.BlockSpec(memory_space=pltpu.SMEM)] + in_vmem(3),
        out_specs=tuple(in_vmem(2)),
        scratch_shapes=[pltpu.VMEM((rows + 8, 128), jnp.int32)],
        name="prep",
    )(counts, order, elem, coords)


def step(request, point, field, channels, sizes):
    peers, _, capacity = request.shape
    rows, elements = field.shape
    width = -(-elements // 256) * 256
    lines, ring, groups = sizes
    messages = groups + lines + ring
    blocks = pltpu.VMEM((peers, channels, capacity), jnp.float32)
    table = pltpu.VMEM((rows + 2 * channels, width), jnp.bfloat16)
    dma = pltpu.SemaphoreType.DMA
    return pl.pallas_call(
        lambda *refs: step_kernel(sizes, *refs),
        out_shape=jax.ShapeDtypeStruct((rows, elements), jnp.float32),
        in_specs=in_vmem(3),
        out_specs=pl.BlockSpec(memory_space=pltpu.VMEM),
        scratch_shapes=[
            pltpu.VMEM((peers, 4, capacity), jnp.float32),
            blocks,
            blocks,
            table,
            table,
            pltpu.VMEM((rows + 2 * channels, 2 * capacity), jnp.float32),
            pltpu.VMEM((rows, width), jnp.float32),
            pltpu.VMEM((2, rows, 2 * capacity), jnp.bfloat16),
            pltpu.VMEM((3, 1, 128), jnp.float32),
            pltpu.VMEM((groups, 1, 128), jnp.float32),
            pltpu.VMEM((lines, 1, 128), jnp.float32),
            pltpu.VMEM((ring, 1, 128), jnp.float32),
            dma((peers,)), dma((peers,)), dma((peers,)), dma((peers,)),
            dma((messages,)), dma((messages,)),
            pltpu.SemaphoreType.REGULAR((8,)),
        ],
        compiler_params=pltpu.CompilerParams(collective_id=0, has_side_effects=True),
        name="step",
    )(request, point, field)


def local(lines, tracers, send_counts, point_order, depart_elem, depart_coords):
    nodes, levels, species, elements = tracers.shape
    channels = levels * species
    groups, capacity = depart_elem.shape[-2:]
    peers = SIDES * groups
    field = tracers.reshape(nodes * channels, elements)
    request, point = prep(
        send_counts.reshape(1, peers),
        point_order.reshape(-1, 128),
        depart_elem.reshape(peers, capacity),
        depart_coords.reshape(2 * peers, capacity),
        elements,
    )
    sizes = (lines, lax.axis_size("sfc") // lines, groups)
    out = step(request, point, field, channels, sizes)
    return out.reshape(nodes, levels, species, elements)


def solution(mesh, lines=4):
    both = ("sfc", "grp")
    return jax.shard_map(
        lambda *args: local(lines, *args),
        mesh=mesh,
        in_specs=(
            P(None, None, None, both),
            P("sfc", "grp", None),
            P("sfc", "grp", None),
            P("sfc", "grp", None, None, None),
            P("sfc", "grp", None, None, None, None),
        ),
        out_specs=P(None, None, None, both),
        check_vma=False,
    )
```

time: 638 us -> 63 us (0.10)
  local copies, waits for them, and re-layouts: 481 us -> 1.88 us
  blocking collectives: 79.3 us -> 0 us
  Pallas kernels: 0 us -> 60.9 us
  starting transfers between devices: 40.8 us -> 0 us
  other arithmetic: 20.5 us -> 0 us
  waiting for transfers between devices: 14.2 us -> 0 us
    gather x51 -> x0, local copies, waits for them, and re-layouts: 430 us -> none  [the longest x32 383 us: interpolate(): jnp.take(tracer_field[4 * row_node + column_node], source_row, axis=1)]
    psum x4 -> x0, blocking collectives: 74.4 us -> none  [over_axes(): x = lax.psum(x, axis)]
    pallas_call x0 -> x2, Pallas kernels: none -> 60.9 us  [the longest x1 59.1 us: step(): pl.pallas_call(lambda *refs: step_kernel(sizes, *refs), out_shape=jax.Sha...]
    ppermute x4 -> x0, starting transfers between devices: 31.9 us -> none  [passed_along(): lax.ppermute(x, axis, [(i, (i + by) % devices) for i in range(devices)])]
    scatter x1 -> x0, local copies, waits for them, and re-layouts: 23 us -> none  [local(): slot_of_point = jnp.zeros((points,), jnp.int32).at[target_point.reshape(-...]
    all_to_all x2 -> x0, waiting for transfers between devices: 14.2 us -> none  [the longest x1 9.21 us: moved_by_axis(): filled = lax.all_to_all(filled, axes[k], k, k, tiled=True)]
    unnamed x63 -> x1, local copies, waits for them, and re-layouts: 15.8 us -> 1.88 us
    all_to_all x2 -> x0, starting transfers between devices: 8.91 us -> none  [the longest x1 5.42 us: local(): lax.all_to_all(stacked, GRP, split_axis=2, concat_axis=2, tiled=True)]
  transfers between devices with their start and end apart: 6 -> 0, of which waited for: 2 -> 0; matrix products, arithmetic and copies ran while one was open for 5% -> 0% of each run, Pallas kernels for 0% -> 0%
where the time goes in v1:
time: 63 us; the launch traced here: 62.8 us
  Pallas kernels  60.9 us (97%)
  local copies, waits for them, and re-layouts  1.88 us (3%)
    pallas_call x1, Pallas kernels, step(): pl.pallas_call(lambda *refs: step_kernel(sizes, *refs), out_shape=jax.Sha...  59.1 us
    unnamed x1, local copies, waits for them, and re-layouts  1.88 us
    pallas_call x1, Pallas kernels, prep(): pl.pallas_call(lambda *refs: prep_kernel(elements, *refs), out_shape=(jax...  1.8 us

profile of v1, /device:TPU:1, one launch (start us, length us, event | category | flops | bytes accessed | tf_op | source)
XLA Modules:
  0.0 62.8 jit_solution(11871540593282518458)
XLA Ops:
  0.0 1.8 %prep.1 = (f32[24,4,256]{2,1,0:T(4,128)}, s32[24,256]{1,0:T(8,128)}) custom-call(s32[1,24]{1,0:T(1,128)} %bitcast.11, s32[24,128]{1,0:T(8,128)} %bitcast.10, s32[24,256]{1,0:T(8,128)} %bitcast.9, f32[48,256]{1,0:T(8,128)} %bitcast.8), custom_call_target="tpu_custom_call" | custom-call | tf_op jit(solution)/shard_map/prep/pallas_call | solution.py:326
  1.8 59.1 %step.1 = f32[512,192]{1,0:T(8,128)} custom-call(f32[24,4,256]{2,1,0:T(4,128)} %get-tuple-element.7.refs_0_, s32[24,256]{1,0:T(8,128)} %get-tuple-element.8.refs_1_, f32[512,192]{1,0:T(8,128)} %bitcast.7), custom_call_target="tpu_custom_call" | custom-call | tf_op jit(solution)/shard_map/step/pallas_call | solution.py:348
  60.9 1.9 %copy.7 = f32[16,4,8,192]{3,2,1,0:T(8,128)} copy(f32[16,4,8,192]{3,2,1,0:T(8,128)} %bitcast.6) | data formatting | bytes 786432

commit v2 on v1

v2 whole, which is shorter than its diff:
```python
import jax
import jax.numpy as jnp
from jax import lax
from jax.experimental import pallas as pl
from jax.experimental.pallas import tpu as pltpu
from jax.sharding import PartitionSpec as P

NODE_COORD = (-1.0, -0.4472135954999579, 0.4472135954999579, 1.0)
SIDES = 3
BATCH = 4
MESH = pl.DeviceIdType.MESH


def lagrange(x):
    values = []
    for i in range(4):
        value = None
        for m in range(4):
            if m != i:
                term = (x - NODE_COORD[m]) * (1.0 / (NODE_COORD[i] - NODE_COORD[m]))
                value = term if value is None else value * term
        values.append(value)
    return values


def line_weight(line):
    return jnp.where((line == 0) | (line == 3), 1.0 / 6.0, 5.0 / 6.0).astype(jnp.float32)


def split_bf16(x):
    high = x.astype(jnp.bfloat16)
    return high, (x - high.astype(jnp.float32)).astype(jnp.bfloat16)


def diagonal(n, start):
    return lax.broadcasted_iota(jnp.int32, (n, 128), 0) + start == lax.broadcasted_iota(
        jnp.int32, (n, 128), 1
    )


def as_row(column, start):
    return jnp.sum(jnp.where(diagonal(column.shape[0], start), column, 0.0), axis=0, keepdims=True)


def as_column(row, n, start):
    return jnp.sum(jnp.where(diagonal(n, start), row, 0.0), axis=1, keepdims=True)


def prepare(elements, counts_ref, order_pad, elem_ref, coord_ref, request_ref, point_ref):
    peers, capacity = elem_ref.shape
    lane = lax.broadcasted_iota(jnp.int32, (8, 128), 1)
    slot = lane + 128 * lax.broadcasted_iota(jnp.int32, (8, 128), 0)
    offset = jnp.int32(0)
    counts, shifts, windows = [], [], []
    for k in range(peers):
        counts.append(counts_ref[0, k])
        shifts.append(jnp.full((8, 128), offset & 127))
        windows.append(order_pad[pl.ds(offset >> 7, 8), :])
        offset = offset + counts[k]
    for bit in range(7):
        step = 1 << bit
        windows = [
            jnp.where((shift & step) != 0, pltpu.roll(window, 128 - step, 1), window)
            for shift, window in zip(shifts, windows)
        ]
    for k in range(peers):
        window = jnp.where(lane < 128 - shifts[k], windows[k], pltpu.roll(windows[k], 7, 0))
        window = jnp.where(slot < counts[k], window, -1)
        for part in range(capacity // 128):
            point_ref[k : k + 1, part * 128 : part * 128 + 128] = window[part : part + 1, :]
    point = point_ref[...]
    node = jnp.floor((point.astype(jnp.float32) + 0.5) * (1.0 / elements)).astype(jnp.int32)
    share = jnp.where(point >= 0, line_weight(node >> 2) * line_weight(node & 3), 0.0)
    element = elem_ref[...].astype(jnp.float32)
    for k in range(peers):
        request_ref[k, 0:1, :] = element[k : k + 1, :]
        request_ref[k, 1:2, :] = coord_ref[k : k + 1, :]
        request_ref[k, 2:3, :] = coord_ref[peers + k : peers + k + 1, :]
        request_ref[k, 3:4, :] = share[k : k + 1, :]


def split_field(field_ref, high_ref, low_ref, channels):
    nodes = field_ref.shape[0] // channels
    elements = field_ref.shape[1]
    rows, width = high_ref.shape
    high_ref[:, 128:] = jnp.zeros((rows, width - 128), jnp.bfloat16)
    low_ref[:, 128:] = jnp.zeros((rows, width - 128), jnp.bfloat16)
    old = least = most = None
    for n in range(nodes):
        plane = field_ref[n * channels : (n + 1) * channels, :]
        weight = (5.0 if n // 4 in (1, 2) else 1.0) * (5.0 if n % 4 in (1, 2) else 1.0) / 36.0
        old = plane * weight if old is None else old + plane * weight
        least = plane if least is None else jnp.minimum(least, plane)
        most = plane if most is None else jnp.maximum(most, plane)
        high, low = split_bf16(plane)
        high_ref[n * channels : (n + 1) * channels, 0:elements] = high
        low_ref[n * channels : (n + 1) * channels, 0:elements] = low
    for n, plane in ((nodes, least), (nodes + 1, most)):
        high, low = split_bf16(plane)
        high_ref[n * channels : (n + 1) * channels, 0:elements] = high
        low_ref[n * channels : (n + 1) * channels, 0:elements] = low
    return jnp.sum(old, axis=1, keepdims=True)


def interpolate(requests, blocks, value_ref, high_ref, low_ref, gathered_ref):
    channels, capacity = value_ref.shape[1:]
    width = high_ref.shape[1]
    nodes = high_ref.shape[0] // channels - 2
    element = jnp.concatenate([requests[b, 0:1, :] for b in blocks], 1).astype(jnp.int32)
    source = lax.broadcasted_iota(jnp.int32, (width, element.shape[1]), 0)
    chosen = jnp.where(source == element, 1.0, 0.0).astype(jnp.bfloat16)
    gathered_ref[...] = jnp.dot(
        high_ref[...], chosen, preferred_element_type=jnp.float32
    ) + jnp.dot(low_ref[...], chosen, preferred_element_type=jnp.float32)
    mass = None
    for i, b in enumerate(blocks):
        cols = slice(i * capacity, (i + 1) * capacity)
        first = lagrange(requests[b, 1:2, :])
        second = lagrange(requests[b, 2:3, :])
        total = None
        for n in range(nodes):
            term = (first[n // 4] * second[n % 4]) * gathered_ref[n * channels : (n + 1) * channels, cols]
            total = term if total is None else total + term
        total = jnp.maximum(total, gathered_ref[nodes * channels : (nodes + 1) * channels, cols])
        total = jnp.minimum(total, gathered_ref[(nodes + 1) * channels : (nodes + 2) * channels, cols])
        value_ref[b] = total
        part = total * requests[b, 3:4, :]
        mass = part if mass is None else mass + part
    return mass


def scatter(point_ref, blocks, returned, total_ref, masked_ref, elements):
    channels, capacity = returned.shape[1:]
    nodes = total_ref.shape[0] // channels
    width = total_ref.shape[1]
    point = jnp.concatenate([point_ref[pl.ds(b, 1), :] for b in blocks], 1)
    node = jnp.floor((point.astype(jnp.float32) + 0.5) * (1.0 / elements)).astype(jnp.int32)
    element = jnp.where(point >= 0, point - node * elements, -1)
    place = lax.broadcasted_iota(jnp.int32, (width, element.shape[1]), 0)
    spread = jnp.where(place == element, 1.0, 0.0).astype(jnp.bfloat16)
    value = jnp.concatenate([returned[b] for b in blocks], 1)
    high, low = split_bf16(value)
    for n in range(nodes):
        mask = jnp.where(node == n, 1.0, 0.0).astype(jnp.bfloat16)
        masked_ref[0, n * channels : (n + 1) * channels, :] = high * mask
        masked_ref[1, n * channels : (n + 1) * channels, :] = low * mask
    dims = (((1,), (1,)), ((), ()))
    total_ref[...] += lax.dot_general(
        masked_ref[0], spread, dims, preferred_element_type=jnp.float32
    ) + lax.dot_general(masked_ref[1], spread, dims, preferred_element_type=jnp.float32)


def step_kernel(
    sizes, counts_hbm, order_hbm, elem_hbm, coord_hbm, field_hbm, total_ref, factor_ref,
    counts_ref, order_pad, elem_ref, coord_ref, field_ref, request_ref, point_ref,
    asked, values, returned, high_ref, low_ref, gathered_ref, masked_ref,
    parts, plane_mass, ring_mass,
    loaded, ask_sent, ask_got, back_sent, back_got, plane_sent, plane_got, ring_sent, ring_got, known,
):
    lines, ring, groups = sizes
    peers, channels, capacity = values.shape
    elements = field_ref.shape[1]
    sfc, grp = lax.axis_index("sfc"), lax.axis_index("grp")
    segments = lines * ring
    line, place = sfc // ring, sfc % ring
    others = peers - 1

    loads = [
        pltpu.make_async_copy(counts_hbm, counts_ref, loaded.at[0]),
        pltpu.make_async_copy(order_hbm, order_pad.at[pl.ds(0, order_hbm.shape[0])], loaded.at[1]),
        pltpu.make_async_copy(elem_hbm, elem_ref, loaded.at[2]),
        pltpu.make_async_copy(coord_hbm, coord_ref, loaded.at[3]),
        pltpu.make_async_copy(field_hbm, field_ref, loaded.at[4]),
    ]
    for load in loads:
        load.start()

    def at(segment, group):
        return {"sfc": segment, "grp": group}

    near = [(sfc + segments + side - 1) % segments for side in range(SIDES)]
    ahead = [(grp + i) % groups for i in range(groups)]
    behind = [(grp + groups - i) % groups for i in range(groups)]

    def side(u):
        return (2 * (u // groups)) % SIDES

    def owner(u):
        if isinstance(u, int):
            return near[side(u)], ahead[(1 + u) % groups]
        return (sfc + side(u) - 1 + segments) % segments, (grp + 1 + u) % groups

    def asker(u):
        if isinstance(u, int):
            return near[SIDES - 1 - side(u)], behind[(1 + u) % groups]
        return (sfc - side(u) + 1 + segments) % segments, (grp - 1 - u + 4 * groups) % groups

    def on_line(i, group):
        return at(((line + i) % lines) * ring + place, group)

    def on_ring(i):
        return at(line * ring + (place + i + ring) % ring, grp)

    def ask(u):
        segment, group = owner(u)
        return pltpu.make_async_remote_copy(
            request_ref.at[side(u) * groups + group],
            asked.at[side(u) * groups + grp],
            ask_sent, ask_got.at[u],
            device_id=at(segment, group), device_id_type=MESH,
        )

    def answer(u):
        segment, group = asker(u)
        return pltpu.make_async_remote_copy(
            values.at[side(u) * groups + group],
            returned.at[side(u) * groups + grp],
            back_sent, back_got.at[u],
            device_id=at(segment, group), device_id_type=MESH,
        )

    def plane_copy(i):
        group = (grp + i) % groups
        return pltpu.make_async_remote_copy(
            parts.at[0], plane_mass.at[line * groups + grp], plane_sent, plane_got,
            device_id=on_line(i // groups, group), device_id_type=MESH,
        )

    def ring_copy(i):
        return pltpu.make_async_remote_copy(
            parts.at[1], ring_mass.at[place], ring_sent, ring_got,
            device_id=on_ring(i), device_id_type=MESH,
        )

    def settle(ref, count, semaphore):
        part = ref.at[pl.ds(0, count)]
        pltpu.make_async_copy(part, part, semaphore).wait()

    barrier = pltpu.get_barrier_semaphore()

    def greet(device):
        pl.semaphore_signal(barrier, inc=1, device_id=device, device_id_type=MESH)

    for u in range(others):
        greet(at(*owner(u)))
    for i in range(1, lines):
        greet(on_line(i, grp))
    for i in (1, -1):
        greet(on_ring(i))

    for load in loads[:4]:
        load.wait()
    prepare(elements, counts_ref, order_pad, elem_ref, coord_ref, request_ref, point_ref)
    asked[groups + grp] = request_ref[groups + grp]

    pl.semaphore_wait(barrier, others + lines - 1 + 2)
    for u in range(others):
        ask(u).start()

    def tell(step):
        for i in (1 << step, -(1 << step)):
            pl.semaphore_signal(known.at[step], inc=1, device_id=on_ring(i), device_id_type=MESH)

    def hear(step):
        pl.semaphore_wait(known.at[step], 2)

    steps = 0
    while (2 << steps) < ring:
        steps += 1
    tell(0)
    loads[4].wait()
    old = split_field(field_ref, high_ref, low_ref, channels)
    for step in range(1, steps - 1):
        hear(step - 1)
        tell(step)
    total_ref[...] = jnp.zeros_like(total_ref)

    plane = lines * groups
    rounds = peers // BATCH
    early = groups
    new = jnp.zeros((channels, capacity), jnp.float32)
    for j in range(rounds):
        batch = range(BATCH * j, BATCH * (j + 1))
        for u in range(BATCH * (j - 1), BATCH * j):
            if 0 <= u < early:
                answer(u).start()
        for u in batch:
            if u < others:
                ask(u).wait_recv()
        blocks = [side(u) * groups + asker(u)[1] for u in batch]
        new = new + interpolate(asked, blocks, values, high_ref, low_ref, gathered_ref)
        if j == rounds // 2:
            hear(steps - 2)
            tell(steps - 1)
    new = jnp.sum(new, axis=1, keepdims=True)
    parts[0] = as_row(old, 0) + as_row(new, channels)
    returned[groups + grp] = values[groups + grp]
    plane_mass[line * groups + grp] = parts[0]
    far = sorted(range(1, plane), key=lambda i: -min(i // groups, lines - i // groups) * groups - min(i % groups, groups - i % groups))
    for i in far:
        plane_copy(i).start()
    for u in range(early, others):
        answer(u).start()
    settle(plane_mass, plane - 1, plane_got)
    parts[1] = jnp.sum(plane_mass[...], axis=0)
    hear(steps - 1)
    ring_mass[place] = parts[1]
    for i in sorted(range(1, ring), key=lambda i: -min(i, ring - i)):
        ring_copy(i).start()

    def put(j, carry):
        for i in range(2):
            @pl.when(2 * j + i < others)
            def _():
                answer(2 * j + i).wait_recv()

        blocks = [side(2 * j + i) * groups + owner(2 * j + i)[1] for i in range(2)]
        scatter(point_ref, blocks, returned, total_ref, masked_ref, elements)
        return carry

    lax.fori_loop(0, peers // 2, put, 0)
    settle(request_ref, others, ask_sent)
    settle(values, others, back_sent)
    settle(plane_mass, plane - 1, plane_sent)
    settle(ring_mass, ring - 1, ring_sent)
    settle(ring_mass, ring - 1, ring_got)
    masses = jnp.sum(ring_mass[...], axis=0)
    factor = as_column(masses, channels, 0) / as_column(masses, channels, channels)
    factor_ref[...] = jnp.broadcast_to(factor, factor_ref.shape)


def step(counts, order, elem, coords, field, channels, sizes):
    peers, capacity = elem.shape
    rows, elements = field.shape
    width = -(-elements // 256) * 256
    lines, ring, groups = sizes
    vmem, dma = pltpu.VMEM, pltpu.SemaphoreType.DMA
    blocks = vmem((peers, channels, capacity), jnp.float32)
    table = vmem((rows + 2 * channels, width), jnp.bfloat16)
    plane = lines * groups
    return pl.pallas_call(
        lambda *refs: step_kernel(sizes, *refs),
        out_shape=(
            jax.ShapeDtypeStruct((rows, width), jnp.float32),
            jax.ShapeDtypeStruct((channels, width), jnp.float32),
        ),
        in_specs=[pl.BlockSpec(memory_space=pltpu.HBM)] * 5,
        out_specs=(pl.BlockSpec(memory_space=pltpu.VMEM),) * 2,
        scratch_shapes=[
            pltpu.SMEM(counts.shape, jnp.int32),
            vmem((order.shape[0] + 8, 128), jnp.int32),
            vmem(elem.shape, jnp.int32),
            vmem(coords.shape, jnp.float32),
            vmem(field.shape, jnp.float32),
            vmem((peers, 4, capacity), jnp.float32),
            vmem((peers, capacity), jnp.int32),
            vmem((peers, 4, capacity), jnp.float32),
            blocks,
            blocks,
            table,
            table,
            vmem((rows + 2 * channels, BATCH * capacity), jnp.float32),
            vmem((2, rows, 2 * capacity), jnp.bfloat16),
            vmem((2, 1, 128), jnp.float32),
            vmem((plane, 1, 128), jnp.float32),
            vmem((ring, 1, 128), jnp.float32),
            dma((5,)),
            dma(()), dma((peers,)), dma(()), dma((peers,)),
            dma(()), dma(()), dma(()), dma(()),
            pltpu.SemaphoreType.REGULAR((8,)),
        ],
        compiler_params=pltpu.CompilerParams(
            collective_id=0, has_side_effects=True, vmem_limit_bytes=24 << 20
        ),
        name="step",
    )(*(pltpu.with_memory_space_constraint(x, pltpu.HBM) for x in (counts, order, elem, coords, field)))


def local(lines, tracers, send_counts, point_order, depart_elem, depart_coords):
    nodes, levels, species, elements = tracers.shape
    channels = levels * species
    groups, capacity = depart_elem.shape[-2:]
    peers = SIDES * groups
    total, factor = step(
        send_counts.reshape(1, peers),
        point_order.reshape(-1, 128),
        depart_elem.reshape(peers, capacity),
        depart_coords.reshape(2 * peers, capacity),
        tracers.reshape(nodes * channels, elements),
        channels,
        (lines, lax.axis_size("sfc") // lines, groups),
    )
    out = total.reshape(nodes, channels, -1)[:, :, :elements] * factor[None, :, :elements]
    return out.reshape(nodes, levels, species, elements)


def solution(mesh, lines=4):
    both = ("sfc", "grp")
    return jax.shard_map(
        lambda *args: local(lines, *args),
        mesh=mesh,
        in_specs=(
            P(None, None, None, both),
            P("sfc", "grp", None),
            P("sfc", "grp", None),
            P("sfc", "grp", None, None, None),
            P("sfc", "grp", None, None, None, None),
        ),
        out_specs=P(None, None, None, both),
        check_vma=False,
    )
```

time: 63 us -> 50.4 us (0.80)
  Pallas kernels: 60.9 us -> 49.4 us
  local copies, waits for them, and re-layouts: 1.88 us -> 0 us
  other arithmetic: 0 us -> 0.84 us
    pallas_call x2 -> x1, Pallas kernels: 60.9 us -> 49.4 us  [step(): pl.pallas_call(lambda *refs: step_kernel(sizes, *refs), out_shape=(jax.Sh...]
    unnamed x1 -> x0, local copies, waits for them, and re-layouts: 1.88 us -> none
    reshape x0 -> x1, other arithmetic: none -> 0.84 us  [local(): return out.reshape(nodes, levels, species, elements)]
where the time goes in v2:
time: 50.4 us; the launch traced here: 50.3 us
  Pallas kernels  49.4 us (98%)
  other arithmetic  0.84 us (2%)
    pallas_call x1, Pallas kernels, step(): pl.pallas_call(lambda *refs: step_kernel(sizes, *refs), out_shape=(jax.Sh...  49.4 us

profile of v2, /device:TPU:1, one launch (start us, length us, event | category | flops | bytes accessed | tf_op | source)
XLA Modules:
  0.0 50.3 jit_solution(2475033407649758939)
XLA Ops:
  0.0 49.4 %step.1 = (f32[512,256]{1,0:T(8,128)S(1)}, f32[32,256]{1,0:T(8,128)S(1)}) custom-call(s32[1,24]{1,0:T(1,128)} %bitcast.15, s32[24,128]{1,0:T(8,128)} %bitcast.14, s32[24,256]{1,0:T(8,128)} %bitcast.13, f32[48,256]{1,0:T(8,128)} %bitcast.12, f32[512,192]{1,0:T(8,128)} %bitcast.11), custom_call_target="tpu_custom_call" | custom-call | tf_op jit(solution)/shard_map/step/pallas_call | solution.py:341
  49.4 0.8 %fusion = f32[16,4,8,192]{3,2,1,0:T(8,128)} fusion(f32[16,32,256]{2,1,0:T(8,128)S(1)} %bitcast.9, f32[32,192]{1,0:T(8,128)S(1)} %bitcast.10), kind=kLoop, calls=%fused_computation.1 | loop fusion | flops 98304 | bytes 811008 | tf_op jit(solution)/shard_map/reshape | solution.py:394

commit v3 on v2

--- a/solution.py
+++ b/solution.py
@@ -299,7 +299,7 @@
     far = sorted(range(1, plane), key=lambda i: -min(i // groups, lines - i // groups) * groups - min(i % groups, groups - i % groups))
     for i in far:
         plane_copy(i).start()
-    for u in range(early, others):
+    for u in range(2 * groups, others):
         answer(u).start()
     settle(plane_mass, plane - 1, plane_got)
     parts[1] = jnp.sum(plane_mass[...], axis=0)
@@ -307,8 +307,12 @@
     ring_mass[place] = parts[1]
     for i in sorted(range(1, ring), key=lambda i: -min(i, ring - i)):
         ring_copy(i).start()
+    for u in range(groups, 2 * groups):
+        answer(u).start()
 
     def put(j, carry):
+        half = groups // 2
+        j = (2 * (j // half)) % SIDES * half + j % half
         for i in range(2):
             @pl.when(2 * j + i < others)
             def _():

time: 50.4 us -> 49.7 us (0.986)
  Pallas kernels: 49.4 us -> 48.7 us
    pallas_call x1, Pallas kernels: 49.4 us -> 48.7 us  [step(): pl.pallas_call(lambda *refs: step_kernel(sizes, *refs), out_shape=(jax.Sh...]
where the time goes in v3:
time: 49.7 us; the launch traced here: 49.6 us
  Pallas kernels  48.7 us (98%)
  other arithmetic  0.84 us (2%)
    pallas_call x1, Pallas kernels, step(): pl.pallas_call(lambda *refs: step_kernel(sizes, *refs), out_shape=(jax.Sh...  48.7 us

profile of v3, /device:TPU:1, one launch (start us, length us, event | category | flops | bytes accessed | tf_op | source)
XLA Modules:
  0.0 49.6 jit_solution(2805891666330646021)
XLA Ops:
  0.0 48.7 %step.1 = (f32[512,256]{1,0:T(8,128)S(1)}, f32[32,256]{1,0:T(8,128)S(1)}) custom-call(s32[1,24]{1,0:T(1,128)} %bitcast.15, s32[24,128]{1,0:T(8,128)} %bitcast.14, s32[24,256]{1,0:T(8,128)} %bitcast.13, f32[48,256]{1,0:T(8,128)} %bitcast.12, f32[512,192]{1,0:T(8,128)} %bitcast.11), custom_call_target="tpu_custom_call" | custom-call | tf_op jit(solution)/shard_map/step/pallas_call | solution.py:345
  48.7 0.8 %fusion = f32[16,4,8,192]{3,2,1,0:T(8,128)} fusion(f32[16,32,256]{2,1,0:T(8,128)S(1)} %bitcast.9, f32[32,192]{1,0:T(8,128)S(1)} %bitcast.10), kind=kLoop, calls=%fused_computation.1 | loop fusion | flops 98304 | bytes 811008 | tf_op jit(solution)/shard_map/reshape | solution.py:398

commit v4 on v2

--- a/solution.py
+++ b/solution.py
@@ -164,6 +164,8 @@
     segments = lines * ring
     line, place = sfc // ring, sfc % ring
     others = peers - 1
+    itself = groups - 1
+    away = [u for u in range(peers) if u != itself]
 
     loads = [
         pltpu.make_async_copy(counts_hbm, counts_ref, loaded.at[0]),
@@ -183,7 +185,7 @@
     behind = [(grp + groups - i) % groups for i in range(groups)]
 
     def side(u):
-        return (2 * (u // groups)) % SIDES
+        return (2 * (u // groups) + 1) % SIDES
 
     def owner(u):
         if isinstance(u, int):
@@ -241,7 +243,7 @@
     def greet(device):
         pl.semaphore_signal(barrier, inc=1, device_id=device, device_id_type=MESH)
 
-    for u in range(others):
+    for u in away:
         greet(at(*owner(u)))
     for i in range(1, lines):
         greet(on_line(i, grp))
@@ -254,7 +256,7 @@
     asked[groups + grp] = request_ref[groups + grp]
 
     pl.semaphore_wait(barrier, others + lines - 1 + 2)
-    for u in range(others):
+    for u in away:
         ask(u).start()
 
     def tell(step):
@@ -282,10 +284,10 @@
     for j in range(rounds):
         batch = range(BATCH * j, BATCH * (j + 1))
         for u in range(BATCH * (j - 1), BATCH * j):
-            if 0 <= u < early:
+            if 0 <= u < early and u != itself:
                 answer(u).start()
         for u in batch:
-            if u < others:
+            if u != itself:
                 ask(u).wait_recv()
         blocks = [side(u) * groups + asker(u)[1] for u in batch]
         new = new + interpolate(asked, blocks, values, high_ref, low_ref, gathered_ref)
@@ -299,7 +301,7 @@
     far = sorted(range(1, plane), key=lambda i: -min(i // groups, lines - i // groups) * groups - min(i % groups, groups - i % groups))
     for i in far:
         plane_copy(i).start()
-    for u in range(early, others):
+    for u in range(groups, 2 * groups):
         answer(u).start()
     settle(plane_mass, plane - 1, plane_got)
     parts[1] = jnp.sum(plane_mass[...], axis=0)
@@ -307,10 +309,12 @@
     ring_mass[place] = parts[1]
     for i in sorted(range(1, ring), key=lambda i: -min(i, ring - i)):
         ring_copy(i).start()
+    for u in range(2 * groups, peers):
+        answer(u).start()
 
     def put(j, carry):
         for i in range(2):
-            @pl.when(2 * j + i < others)
+            @pl.when(2 * j + i != itself)
             def _():
                 answer(2 * j + i).wait_recv()
 

time: 50.4 us -> 49.4 us (0.980)
  Pallas kernels: 49.4 us -> 48.4 us
    pallas_call x1, Pallas kernels: 49.4 us -> 48.4 us  [step(): pl.pallas_call(lambda *refs: step_kernel(sizes, *refs), out_shape=(jax.Sh...]
where the time goes in v4:
time: 49.4 us; the launch traced here: 49.3 us
  Pallas kernels  48.4 us (98%)
  other arithmetic  0.84 us (2%)
    pallas_call x1, Pallas kernels, step(): pl.pallas_call(lambda *refs: step_kernel(sizes, *refs), out_shape=(jax.Sh...  48.4 us

profile of v4, /device:TPU:1, one launch (start us, length us, event | category | flops | bytes accessed | tf_op | source)
XLA Modules:
  0.0 49.3 jit_solution(3922948331826248732)
XLA Ops:
  0.0 48.4 %step.1 = (f32[512,256]{1,0:T(8,128)S(1)}, f32[32,256]{1,0:T(8,128)S(1)}) custom-call(s32[1,24]{1,0:T(1,128)} %bitcast.15, s32[24,128]{1,0:T(8,128)} %bitcast.14, s32[24,256]{1,0:T(8,128)} %bitcast.13, f32[48,256]{1,0:T(8,128)} %bitcast.12, f32[512,192]{1,0:T(8,128)} %bitcast.11), custom_call_target="tpu_custom_call" | custom-call | tf_op jit(solution)/shard_map/step/pallas_call | solution.py:345
  48.4 0.8 %fusion = f32[16,4,8,192]{3,2,1,0:T(8,128)} fusion(f32[16,32,256]{2,1,0:T(8,128)S(1)} %bitcast.9, f32[32,192]{1,0:T(8,128)S(1)} %bitcast.10), kind=kLoop, calls=%fused_computation.1 | loop fusion | flops 98304 | bytes 811008 | tf_op jit(solution)/shard_map/reshape | solution.py:398
